TPU v7x, 128 devices: a whole 4x4x4 slice. The times are simulated.
128 devices in a mesh: row: 8 (over z, core), col: 16 (over y, x).
Axes of the slice: x: 4, y: 4, z: 4, core: 2. Of those that a mesh axis runs over, the one named last changes fastest.
Arguments:
- grad_out: bfloat16 [131072, 256], P(('row', 'col')), may hold values from -6 to 6
- rel_weight: bfloat16 [4, 256, 256], replicated, may hold values from -0.375 to 0.375
- adjacency: bfloat16 [24576, 128, 128], P(('row', 'col')), may hold values from -0.5 to 0.5
- block_row: int32 [24576], P(('row', 'col')), may hold values from 0 to 127, as said below
- block_col: int32 [24576], P(('row', 'col')), may hold values from 0 to 63
- type_count: int32 [512], P(('row', 'col')), may hold values from 0 to 192, as said below
Outputs:
- grad_in: float32 [131072, 256], P(('row', 'col'))
Inputs may be any that keep to these rules, and one draw needn't show every extreme that they name: `block_row`: among all 192 slots of one tile, at most 4 distinct values fall in any aligned range of 8 values (the node blocks of one device of the tile row), and in every tile some range holds exactly 4. `type_count`: A tile's 4 counts sum to at most 192; in some tile a single type holds all 192 slots.
All inputs are finite; a program needn't handle non-finite values.
Results may differ from a plain program's by a relative error of at most 0.012.
Values may be sent and summed in bfloat16 or wider, within the bound.
A program may use at most 192 MiB of HBM per device.

v0:
```python
import math
import jax
import jax.numpy as jnp
from jax import lax
from jax.sharding import PartitionSpec as P


def per_device(grad_out, rel_weight, adjacency, block_row, block_col, type_count):
    ncols = lax.axis_size("col")
    nrows = lax.axis_size("row")
    blk = adjacency.shape[1]
    feat = grad_out.shape[1]
    kinds = rel_weight.shape[0]
    owned = grad_out.shape[0] // blk
    slots_total = adjacency.shape[0]
    wcat = jnp.transpose(rel_weight, (2, 0, 1)).reshape(feat, kinds * feat)
    gathered = jnp.dot(
        lax.all_gather(grad_out, "col", axis=0, tiled=True),
        wcat,
        preferred_element_type=jnp.float32,
    ).astype(jnp.bfloat16)
    table = gathered.reshape(ncols * owned, blk, kinds, feat)
    ends = jnp.cumsum(type_count)
    total = ends[kinds - 1]
    position = jnp.arange(slots_total, dtype=jnp.int32)
    kind = jnp.minimum(
        jnp.sum((position[:, None] >= ends[None, :]).astype(jnp.int32), axis=1), kinds - 1
    )
    live = position < total
    group = math.gcd(slots_total, 64)
    groups = slots_total // group
    partial_start = jnp.zeros((nrows * owned, blk, feat), jnp.float32)

    def step(index, partial_value):
        start = index * group
        adj_part = lax.dynamic_slice_in_dim(adjacency, start, group, 0)
        slot_part = lax.dynamic_slice_in_dim(block_row, start, group, 0)
        kind_part = lax.dynamic_slice_in_dim(kind, start, group, 0)
        live_part = lax.dynamic_slice_in_dim(live, start, group, 0)
        col_part = lax.dynamic_slice_in_dim(block_col, start, group, 0)
        picked = table[slot_part, :, kind_part, :]
        term = jnp.einsum("kab,kaf->kbf", adj_part, picked, preferred_element_type=jnp.float32)
        term = jnp.where(live_part[:, None, None], term, jnp.float32(0.0))
        return partial_value.at[col_part].add(term)

    partial_value = lax.fori_loop(0, groups, step, partial_start)
    return lax.psum_scatter(
        partial_value.reshape(nrows * owned * blk, feat).astype(jnp.bfloat16),
        "row",
        scatter_dimension=0,
        tiled=True,
    ).astype(jnp.float32)


def solution(mesh):
    in_specs = (
        P(("row", "col"), None),
        P(),
        P(("row", "col"), None, None),
        P(("row", "col")),
        P(("row", "col")),
        P(("row", "col")),
    )
    out_specs = P(("row", "col"), None)
    return jax.shard_map(
        per_device, mesh=mesh, in_specs=in_specs, out_specs=out_specs, check_vma=False
    )
```

profile of v0, /device:TPU:0, one launch (start us, length us, event | category | flops | bytes accessed | tf_op | source)
XLA Modules:
  0.0 332.7 jit_solution(6268306720380920505)
XLA Ops:
  6.5 0.0 all-gather.2.cloned.1.call-start
  6.5 0.7 all-gather.2.cloned.1.call-update
  7.3 0.0 reduce-scatter.2.cloned.1.call-start
  7.3 0.8 reduce-window.4
  8.1 0.6 slice.4
  8.7 0.6 iota_compare_fusion.1
  9.3 0.1 convert_reduce_fusion
  9.4 73.3 %all-gather.2.cloned.1.call-done = bf16[16384,256]{1,0:T(8,128)(2,1)} async-done(((bf16[1024,256]{1,0:T(8,128)(2,1)}), bf16[16384,256]{1,0:T(8,128)(2,1)}) %all-gather.2.cloned.1.call-update) | async-done | bytes 8388624 | tf_op jit(solution)/shard_map/all_gather | solution.py:18
  82.7 17.5 %convolution_convert_fusion = bf16[16384,1024]{1,0:T(8,128)(2,1)} fusion(bf16[16384,256]{1,0:T(8,128)(2,1)} %all-gather.2.cloned.1.call-done, bf16[256,1024]{0,1:T(8,128)(2,1)S(1)} %bitcast.12), kind=kOutput, calls=%fused_computation.13 | convolution fusion | flops 8606711808 | bytes 42467328 | tf_op jit(solution)/shard_map/dot_general | solution.py:17
  100.1 54.7 %reshape.19 = bf16[128,128,4,256]{3,2,1,0:T(4,128)(2,1)} reshape(bf16[16384,1024]{1,0:T(8,128)(2,1)} %convolution_convert_fusion) | data formatting | bytes 67108864 | tf_op jit(solution)/shard_map/reshape | solution.py:22
  154.8 23.0 %copy.12 = bf16[128,128,4,256]{3,1,2,0:T(8,128)(2,1)} copy(bf16[128,128,4,256]{3,2,1,0:T(4,128)(2,1)} %reshape.19) | data formatting | bytes 67108864 | tf_op jit(solution)/shard_map/while | solution.py:46
  177.9 4.2 %broadcast_in_dim.53 = f32[64,128,256]{2,1,0:T(8,128)} broadcast(f32[]{:T(128)} %constant.55.clone.1), dimensions={} | broadcast | bytes 8388612 | tf_op jit(solution)/shard_map/broadcast_in_dim | solution.py:32
  182.1 97.6 %while.13 = (s32[]{:T(128)}, f32[64,128,256]{2,1,0:T(8,128)}, s32[192]{0:T(256)S(1)}, pred[192]{0:T(512)(128)(4,1)S(1)}, bf16[192,128,128]{2,1,0:T(8,128)(2,1)},...) while((s32[]{:T(128)}, f32[64,128,256]{2,1,0:T(8,128)}, ...), condition=%wide.region_4.5_spmd, body=%wide.region_2.4_spmd.sunk | while | flops 541066112 | bytes 48236912 | solution.py:46
  182.1 0.1 compare_select_fusion.4
  182.2 5.2 %gather_fusion = bf16[64,128,256]{2,1,0:T(8,128)(2,1)} fusion(bf16[128,128,4,256]{3,1,2,0:T(8,128)(2,1)} %get-tuple-element.271, s32[64]{0:T(128)S(1)} %get-tuple-element.239), kind=kCustom, calls=%fused_computation.clone.1 | custom fusion | bytes 8389120 | tf_op jit(solution)/shard_map/while/body/eval_jaxpr/gather | solution.py:41
  187.3 0.1 dynamic_slice.45
  187.4 7.6 %broadcast_select_fusion.2 = f32[64,128,256]{2,1,0:T(8,128)} fusion(pred[64]{0:T(512)(128)(4,1)S(1)} %dynamic_slice.45, bf16[64,128,256]{2,1,0:T(8,128)(2,1)} %gather_fusion, bf16[192,128,128]{2,1,0:T(8,128)(2,1)} %get-tuple-element.268, s32[]{:T(128)S(6)} %select_n.61), kind=kOutput, calls=%fused_computation.2.clone.1 | convolution fusion | flops 538968064 | bytes 14680132 | tf_op jit(solution)/shard_map/while/body/eval_jaxpr/kab,kaf->kbf/dot_general | solution.py:42
  195.0 19.6 %scatter_fusion = f32[64,128,256]{2,1,0:T(8,128)} fusion(f32[64,128,256]{2,1,0:T(8,128)} %get-tuple-element.253, s32[64]{0:T(128)S(1)} %get-tuple-element.238, f32[64,128,256]{2,1,0:T(8,128)} %broadcast_select_fusion.2), kind=kCustom, calls=%fused_computation.1.clone.1 | custom fusion | flops 2097152 | bytes 25166080 | tf_op jit(solution)/shard_map/while/body/eval_jaxpr/scatter-add | solution.py:44
  214.6 0.1 compare_select_fusion.4
  214.7 5.4 %gather_fusion = bf16[64,128,256]{2,1,0:T(8,128)(2,1)} fusion(bf16[128,128,4,256]{3,1,2,0:T(8,128)(2,1)} %get-tuple-element.271, s32[64]{0:T(128)S(1)} %get-tuple-element.239), kind=kCustom, calls=%fused_computation.clone.1 | custom fusion | bytes 8389120 | tf_op jit(solution)/shard_map/while/body/eval_jaxpr/gather | solution.py:41
  220.1 0.1 dynamic_slice.45
  220.2 7.6 %broadcast_select_fusion.2 = f32[64,128,256]{2,1,0:T(8,128)} fusion(pred[64]{0:T(512)(128)(4,1)S(1)} %dynamic_slice.45, bf16[64,128,256]{2,1,0:T(8,128)(2,1)} %gather_fusion, bf16[192,128,128]{2,1,0:T(8,128)(2,1)} %get-tuple-element.268, s32[]{:T(128)S(6)} %select_n.61), kind=kOutput, calls=%fused_computation.2.clone.1 | convolution fusion | flops 538968064 | bytes 14680132 | tf_op jit(solution)/shard_map/while/body/eval_jaxpr/kab,kaf->kbf/dot_general | solution.py:42
  227.8 19.6 %scatter_fusion = f32[64,128,256]{2,1,0:T(8,128)} fusion(f32[64,128,256]{2,1,0:T(8,128)} %get-tuple-element.253, s32[64]{0:T(128)S(1)} %get-tuple-element.238, f32[64,128,256]{2,1,0:T(8,128)} %broadcast_select_fusion.2), kind=kCustom, calls=%fused_computation.1.clone.1 | custom fusion | flops 2097152 | bytes 25166080 | tf_op jit(solution)/shard_map/while/body/eval_jaxpr/scatter-add | solution.py:44
  247.3 0.1 compare_select_fusion.4
  247.4 5.3 %gather_fusion = bf16[64,128,256]{2,1,0:T(8,128)(2,1)} fusion(bf16[128,128,4,256]{3,1,2,0:T(8,128)(2,1)} %get-tuple-element.271, s32[64]{0:T(128)S(1)} %get-tuple-element.239), kind=kCustom, calls=%fused_computation.clone.1 | custom fusion | bytes 8389120 | tf_op jit(solution)/shard_map/while/body/eval_jaxpr/gather | solution.py:41
  252.7 0.1 dynamic_slice.45
  252.8 7.6 %broadcast_select_fusion.2 = f32[64,128,256]{2,1,0:T(8,128)} fusion(pred[64]{0:T(512)(128)(4,1)S(1)} %dynamic_slice.45, bf16[64,128,256]{2,1,0:T(8,128)(2,1)} %gather_fusion, bf16[192,128,128]{2,1,0:T(8,128)(2,1)} %get-tuple-element.268, s32[]{:T(128)S(6)} %select_n.61), kind=kOutput, calls=%fused_computation.2.clone.1 | convolution fusion | flops 538968064 | bytes 14680132 | tf_op jit(solution)/shard_map/while/body/eval_jaxpr/kab,kaf->kbf/dot_general | solution.py:42
  260.3 19.4 %scatter_fusion = f32[64,128,256]{2,1,0:T(8,128)} fusion(f32[64,128,256]{2,1,0:T(8,128)} %get-tuple-element.253, s32[64]{0:T(128)S(1)} %get-tuple-element.238, f32[64,128,256]{2,1,0:T(8,128)} %broadcast_select_fusion.2), kind=kCustom, calls=%fused_computation.1.clone.1 | custom fusion | flops 2097152 | bytes 25166080 | tf_op jit(solution)/shard_map/while/body/eval_jaxpr/scatter-add | solution.py:44
  279.7 6.0 %convert_element_type.17 = bf16[64,128,256]{2,1,0:T(8,128)(2,1)} convert(f32[64,128,256]{2,1,0:T(8,128)} %get-tuple-element.144) | non-fusion elementwise | flops 2097152 | bytes 12582912 | tf_op jit(solution)/shard_map/convert_element_type | solution.py:48
  285.7 0.0 reduce-scatter.2.cloned.1.call-update
  285.8 38.0 %reduce-scatter.2.cloned.1.call-done = bf16[1024,256]{1,0:T(8,128)(2,1)} async-done(((bf16[8192,256]{1,0:T(8,128)(2,1)}), bf16[1024,256]{1,0:T(8,128)(2,1)}) %reduce-scatter.2.cloned.1.call-update) | async-done | bytes 524304 | tf_op jit(solution)/shard_map/reduce_scatter | solution.py:47
  323.8 2.1 convert_element_type.19
  (9 shorter events, 0.0 us)
Async XLA Ops:
  6.5 76.1 %copy-start = (bf16[4,256,256]{2,1,0:T(8,128)(2,1)S(1)}, bf16[4,256,256]{2,1,0:T(8,128)(2,1)}, u32[]{:S(2)}) copy-start(bf16[4,256,256]{2,1,0:T(8,128)(2,1)} %param.9) | copy-start | bytes 1572868
  6.5 76.1 %all-gather.2.cloned.1.call-start = ((), (), s32[]{:S(2)}) async-start(), calls=%async_computation.1 | async-start | bytes 8912896 | tf_op jit(solution)/shard_map/all_gather | solution.py:18
  7.3 316.5 %reduce-scatter.2.cloned.1.call-start = ((), (), s32[]{:S(2)}) async-start(), calls=%async_computation.2 | async-start | bytes 4718592 | tf_op jit(solution)/shard_map/reduce_scatter | solution.py:47
  177.9 4.2 %copy-start.2 = (s32[192]{0:T(256)S(1)}, s32[192]{0:T(256)}, u32[]{:S(2)}) copy-start(s32[192]{0:T(256)} %param.12) | copy-start | bytes 2308
  177.9 4.2 %copy-start.3 = (s32[192]{0:T(256)S(1)}, s32[192]{0:T(256)}, u32[]{:S(2)}) copy-start(s32[192]{0:T(256)} %param.11) | copy-start | bytes 2308
  279.7 46.1 %copy-start.1 = (bf16[4,256,256]{2,1,0:T(8,128)(2,1)S(1)}, bf16[4,256,256]{2,1,0:T(8,128)(2,1)}, u32[]{:S(2)}) copy-start(bf16[4,256,256]{2,1,0:T(8,128)(2,1)} %param.9) | copy-start | bytes 1572868
Sparse Core Ops, SparseCore 0:
  9.5 73.1 all-gather.1
  285.9 37.8 reduce-scatter.1
where the time goes:
time: 335 us; the launch traced here: 333 us
  waiting for transfers between devices  112 us (33%)
  local copies, waits for them, and re-layouts  98.6 us (29%)
  other arithmetic  68.4 us (20%)
  matrix products  40.1 us (12%)
  between operations  13.4 us (4%)
    all_gather x1, waiting for transfers between devices, per_device(): lax.all_gather(grad_out, 'col', axis=0, tiled=True)  73.3 us
    scatter-add x3, other arithmetic, step(): return partial_value.at[col_part].add(term)  58.6 us
    reshape x1, local copies, waits for them, and re-layouts, per_device(): table = gathered.reshape(ncols * owned, blk, kinds, feat)  54.7 us
    reduce_scatter x1, waiting for transfers between devices, per_device(): lax.psum_scatter(partial_value.reshape(nrows * owned * blk, feat).astype(...  38 us
    while x1, local copies, waits for them, and re-layouts, per_device(): partial_value = lax.fori_loop(0, groups, step, partial_start)  23 us
    dot_general x3, matrix products, step(): jnp.einsum('kab,kaf->kbf', adj_part, picked, preferred_element_type=jnp.f...  22.7 us
    dot_general x1, matrix products, per_device(): jnp.dot(lax.all_gather(grad_out, 'col', axis=0, tiled=True), wcat, prefer...  17.5 us
    gather x3, local copies, waits for them, and re-layouts, step(): picked = table[slot_part, :, kind_part, :]  15.9 us
  transfers between devices with their start and end apart: 2, of which 2 were waited for; matrix products, arithmetic and copies ran while one was open for 1% of the time, Pallas kernels for 0%

commit v1 on v0

--- a/solution.py
+++ b/solution.py
@@ -15,7 +15,9 @@
     slots_total = adjacency.shape[0]
     wcat = jnp.transpose(rel_weight, (2, 0, 1)).reshape(feat, kinds * feat)
     gathered = jnp.dot(
-        lax.all_gather(grad_out, "col", axis=0, tiled=True),
+        jnp.concatenate(
+            lax.all_to_all(jnp.stack([grad_out] * lax.axis_size("col")), "col", 0, 0), axis=0
+        ),
         wcat,
         preferred_element_type=jnp.float32,
     ).astype(jnp.bfloat16)

time: 335 us -> 396 us (1.18)
  waiting for transfers between devices: 112 us -> 162 us
  starting transfers between devices: 0.04 us -> 7.37 us
  local copies, waits for them, and re-layouts: 98.6 us -> 104 us
    all_to_all x0 -> x1, waiting for transfers between devices: none -> 123 us  [per_device(): lax.all_to_all(jnp.stack([grad_out] * lax.axis_size('col')), 'col', 0, 0)]
    all_gather x1 -> x0, waiting for transfers between devices: 73.3 us -> none  [per_device(): lax.all_gather(grad_out, 'col', axis=0, tiled=True)]
    all_to_all x0 -> x1, starting transfers between devices: none -> 7.33 us  [per_device(): lax.all_to_all(jnp.stack([grad_out] * lax.axis_size('col')), 'col', 0, 0)]
    another operation x0 -> x1, local copies, waits for them, and re-layouts: none -> 5.12 us  [per_device(): jnp.stack([grad_out] * lax.axis_size('col'))]
  transfers between devices with their start and end apart: 2 -> 2, of which waited for: 2 -> 2; matrix products, arithmetic and copies ran while one was open for 1% -> 0% of each run, Pallas kernels for 0% -> 0%
where the time goes in v1:
time: 396 us; the launch traced here: 394 us
  waiting for transfers between devices  162 us (41%)
  local copies, waits for them, and re-layouts  104 us (26%)
  other arithmetic  67.9 us (17%)
  matrix products  40.1 us (10%)
  between operations  13.4 us (3%)
  starting transfers between devices  7.37 us (2%)
    all_to_all x1, waiting for transfers between devices, per_device(): lax.all_to_all(jnp.stack([grad_out] * lax.axis_size('col')), 'col', 0, 0)  123 us
    scatter-add x3, other arithmetic, step(): return partial_value.at[col_part].add(term)  58.6 us
    reshape x1, local copies, waits for them, and re-layouts, per_device(): table = gathered.reshape(ncols * owned, blk, kinds, feat)  54.7 us
    reduce_scatter x1, waiting for transfers between devices, per_device(): lax.psum_scatter(partial_value.reshape(nrows * owned * blk, feat).astype(...  38.9 us
    while x1, local copies, waits for them, and re-layouts, per_device(): partial_value = lax.fori_loop(0, groups, step, partial_start)  23 us
    dot_general x3, matrix products, step(): jnp.einsum('kab,kaf->kbf', adj_part, picked, preferred_element_type=jnp.f...  22.7 us
    dot_general x1, matrix products, per_device(): jnp.dot(jnp.concatenate(lax.all_to_all(jnp.stack([grad_out] * lax.axis_si...  17.5 us
    gather x3, local copies, waits for them, and re-layouts, step(): picked = table[slot_part, :, kind_part, :]  15.9 us
  transfers between devices with their start and end apart: 2, of which 2 were waited for; matrix products, arithmetic and copies ran while one was open for 0% of the time, Pallas kernels for 0%

profile of v1, /device:TPU:0, one launch (start us, length us, event | category | flops | bytes accessed | tf_op | source)
XLA Modules:
  0.0 394.1 jit_solution(15003053328651732664)
XLA Ops:
  6.5 5.1 %stack.2 = bf16[16,1024,256]{2,1,0:T(8,128)(2,1)} broadcast(bf16[1024,256]{1,0:T(8,128)(2,1)} %param.8), dimensions={1,2} | broadcast | bytes 8912896 | tf_op jit(solution)/shard_map/stack | solution.py:19
  11.7 7.3 %all-to-all-start = ((bf16[16,1024,256]{2,1,0:T(8,128)(2,1)}), bf16[16,1024,256]{2,1,0:T(8,128)(2,1)}, u32[]{:S(2)}, u32[]{:S(2)}) async-start(bf16[16,1024,256]{2,1,0:T(8,128)(2,1)} %stack.2), calls=%async_computation | async-start | bytes 16777216 | tf_op jit(solution)/shard_map/all_to_all | solution.py:19
  19.0 0.0 reduce-scatter.2.cloned.1.call-start
  19.1 0.2 reduce-window.4
  19.2 0.6 slice.4
  19.8 0.6 iota_compare_fusion.1
  20.5 0.1 convert_reduce_fusion
  20.6 122.6 %all-to-all-done = bf16[16,1024,256]{2,1,0:T(8,128)(2,1)} async-done(((bf16[16,1024,256]{2,1,0:T(8,128)(2,1)}), bf16[16,1024,256]{2,1,0:T(8,128)(2,1)}, u32[]{:S(2)}, u32[]{:S(2)}) %all-to-all-start) | async-done | bytes 8388640 | tf_op jit(solution)/shard_map/all_to_all | solution.py:19
  143.2 17.5 %convolution_convert_fusion = bf16[16384,1024]{1,0:T(8,128)(2,1)} fusion(bf16[16384,256]{1,0:T(8,128)(2,1)} %bitcast.3, bf16[256,1024]{0,1:T(8,128)(2,1)S(1)} %bitcast.13), kind=kOutput, calls=%fused_computation.13 | convolution fusion | flops 8606711808 | bytes 42467328 | tf_op jit(solution)/shard_map/dot_general | solution.py:17
  160.6 54.7 %reshape.25 = bf16[128,128,4,256]{3,2,1,0:T(4,128)(2,1)} reshape(bf16[16384,1024]{1,0:T(8,128)(2,1)} %convolution_convert_fusion) | data formatting | bytes 67108864 | tf_op jit(solution)/shard_map/reshape | solution.py:24
  215.3 23.0 %copy.12 = bf16[128,128,4,256]{3,1,2,0:T(8,128)(2,1)} copy(bf16[128,128,4,256]{3,2,1,0:T(4,128)(2,1)} %reshape.25) | data formatting | bytes 67108864 | tf_op jit(solution)/shard_map/while | solution.py:48
  238.3 4.2 %broadcast_in_dim.53 = f32[64,128,256]{2,1,0:T(8,128)} broadcast(f32[]{:T(128)} %constant.55.clone.1), dimensions={} | broadcast | bytes 8388612 | tf_op jit(solution)/shard_map/broadcast_in_dim | solution.py:34
  242.6 97.6 %while.13 = (s32[]{:T(128)}, f32[64,128,256]{2,1,0:T(8,128)}, s32[192]{0:T(256)S(1)}, pred[192]{0:T(512)(128)(4,1)S(1)}, bf16[192,128,128]{2,1,0:T(8,128)(2,1)},...) while((s32[]{:T(128)}, f32[64,128,256]{2,1,0:T(8,128)}, ...), condition=%wide.region_4.5_spmd, body=%wide.region_2.4_spmd.sunk | while | flops 541066112 | bytes 48236912 | solution.py:48
  242.6 0.1 compare_select_fusion.4
  242.7 5.2 %gather_fusion = bf16[64,128,256]{2,1,0:T(8,128)(2,1)} fusion(bf16[128,128,4,256]{3,1,2,0:T(8,128)(2,1)} %get-tuple-element.271, s32[64]{0:T(128)S(1)} %get-tuple-element.239), kind=kCustom, calls=%fused_computation.clone.1 | custom fusion | bytes 8389120 | tf_op jit(solution)/shard_map/while/body/eval_jaxpr/gather | solution.py:43
  247.8 0.1 dynamic_slice.45
  247.9 7.6 %broadcast_select_fusion.2 = f32[64,128,256]{2,1,0:T(8,128)} fusion(pred[64]{0:T(512)(128)(4,1)S(1)} %dynamic_slice.45, bf16[64,128,256]{2,1,0:T(8,128)(2,1)} %gather_fusion, bf16[192,128,128]{2,1,0:T(8,128)(2,1)} %get-tuple-element.268, s32[]{:T(128)S(6)} %select_n.61), kind=kOutput, calls=%fused_computation.2.clone.1 | convolution fusion | flops 538968064 | bytes 14680132 | tf_op jit(solution)/shard_map/while/body/eval_jaxpr/kab,kaf->kbf/dot_general | solution.py:44
  255.5 19.6 %scatter_fusion = f32[64,128,256]{2,1,0:T(8,128)} fusion(f32[64,128,256]{2,1,0:T(8,128)} %get-tuple-element.253, s32[64]{0:T(128)S(1)} %get-tuple-element.238, f32[64,128,256]{2,1,0:T(8,128)} %broadcast_select_fusion.2), kind=kCustom, calls=%fused_computation.1.clone.1 | custom fusion | flops 2097152 | bytes 25166080 | tf_op jit(solution)/shard_map/while/body/eval_jaxpr/scatter-add | solution.py:46
  275.1 0.1 compare_select_fusion.4
  275.2 5.4 %gather_fusion = bf16[64,128,256]{2,1,0:T(8,128)(2,1)} fusion(bf16[128,128,4,256]{3,1,2,0:T(8,128)(2,1)} %get-tuple-element.271, s32[64]{0:T(128)S(1)} %get-tuple-element.239), kind=kCustom, calls=%fused_computation.clone.1 | custom fusion | bytes 8389120 | tf_op jit(solution)/shard_map/while/body/eval_jaxpr/gather | solution.py:43
  280.6 0.1 dynamic_slice.45
  280.7 7.6 %broadcast_select_fusion.2 = f32[64,128,256]{2,1,0:T(8,128)} fusion(pred[64]{0:T(512)(128)(4,1)S(1)} %dynamic_slice.45, bf16[64,128,256]{2,1,0:T(8,128)(2,1)} %gather_fusion, bf16[192,128,128]{2,1,0:T(8,128)(2,1)} %get-tuple-element.268, s32[]{:T(128)S(6)} %select_n.61), kind=kOutput, calls=%fused_computation.2.clone.1 | convolution fusion | flops 538968064 | bytes 14680132 | tf_op jit(solution)/shard_map/while/body/eval_jaxpr/kab,kaf->kbf/dot_general | solution.py:44
  288.2 19.6 %scatter_fusion = f32[64,128,256]{2,1,0:T(8,128)} fusion(f32[64,128,256]{2,1,0:T(8,128)} %get-tuple-element.253, s32[64]{0:T(128)S(1)} %get-tuple-element.238, f32[64,128,256]{2,1,0:T(8,128)} %broadcast_select_fusion.2), kind=kCustom, calls=%fused_computation.1.clone.1 | custom fusion | flops 2097152 | bytes 25166080 | tf_op jit(solution)/shard_map/while/body/eval_jaxpr/scatter-add | solution.py:46
  307.8 0.1 compare_select_fusion.4
  307.9 5.3 %gather_fusion = bf16[64,128,256]{2,1,0:T(8,128)(2,1)} fusion(bf16[128,128,4,256]{3,1,2,0:T(8,128)(2,1)} %get-tuple-element.271, s32[64]{0:T(128)S(1)} %get-tuple-element.239), kind=kCustom, calls=%fused_computation.clone.1 | custom fusion | bytes 8389120 | tf_op jit(solution)/shard_map/while/body/eval_jaxpr/gather | solution.py:43
  313.2 0.1 dynamic_slice.45
  313.2 7.6 %broadcast_select_fusion.2 = f32[64,128,256]{2,1,0:T(8,128)} fusion(pred[64]{0:T(512)(128)(4,1)S(1)} %dynamic_slice.45, bf16[64,128,256]{2,1,0:T(8,128)(2,1)} %gather_fusion, bf16[192,128,128]{2,1,0:T(8,128)(2,1)} %get-tuple-element.268, s32[]{:T(128)S(6)} %select_n.61), kind=kOutput, calls=%fused_computation.2.clone.1 | convolution fusion | flops 538968064 | bytes 14680132 | tf_op jit(solution)/shard_map/while/body/eval_jaxpr/kab,kaf->kbf/dot_general | solution.py:44
  320.8 19.4 %scatter_fusion = f32[64,128,256]{2,1,0:T(8,128)} fusion(f32[64,128,256]{2,1,0:T(8,128)} %get-tuple-element.253, s32[64]{0:T(128)S(1)} %get-tuple-element.238, f32[64,128,256]{2,1,0:T(8,128)} %broadcast_select_fusion.2), kind=kCustom, calls=%fused_computation.1.clone.1 | custom fusion | flops 2097152 | bytes 25166080 | tf_op jit(solution)/shard_map/while/body/eval_jaxpr/scatter-add | solution.py:46
  340.2 6.0 %convert_element_type.17 = bf16[64,128,256]{2,1,0:T(8,128)(2,1)} convert(f32[64,128,256]{2,1,0:T(8,128)} %get-tuple-element.144) | non-fusion elementwise | flops 2097152 | bytes 12582912 | tf_op jit(solution)/shard_map/convert_element_type | solution.py:50
  346.2 0.0 reduce-scatter.2.cloned.1.call-update
  346.2 38.9 %reduce-scatter.2.cloned.1.call-done = bf16[1024,256]{1,0:T(8,128)(2,1)} async-done(((bf16[8192,256]{1,0:T(8,128)(2,1)}), bf16[1024,256]{1,0:T(8,128)(2,1)}) %reduce-scatter.2.cloned.1.call-update) | async-done | bytes 524304 | tf_op jit(solution)/shard_map/reduce_scatter | solution.py:49
  385.2 2.1 convert_element_type.19
  (11 shorter events, 0.0 us)
Async XLA Ops:
  6.5 136.6 %copy-start = (bf16[4,256,256]{2,1,0:T(8,128)(2,1)S(1)}, bf16[4,256,256]{2,1,0:T(8,128)(2,1)}, u32[]{:S(2)}) copy-start(bf16[4,256,256]{2,1,0:T(8,128)(2,1)} %param.9) | copy-start | bytes 1572868
  11.7 7.4 %copy-start.4 = (s32[4]{0:T(128)S(1)}, s32[4]{0:T(128)}, u32[]{:S(2)}) copy-start(s32[4]{0:T(128)} %param.13) | copy-start | bytes 52
  11.7 131.5 %all-to-all-start = ((bf16[16,1024,256]{2,1,0:T(8,128)(2,1)}), bf16[16,1024,256]{2,1,0:T(8,128)(2,1)}, u32[]{:S(2)}, u32[]{:S(2)}) async-start(bf16[16,1024,256]{2,1,0:T(8,128)(2,1)} %stack.2), calls=%async_computation | async-start | bytes 16777216 | tf_op jit(solution)/shard_map/all_to_all | solution.py:19
  19.0 366.2 %reduce-scatter.2.cloned.1.call-start = ((), (), s32[]{:S(2)}) async-start(), calls=%async_computation.2 | async-start | bytes 4718592 | tf_op jit(solution)/shard_map/reduce_scatter | solution.py:49
  238.3 4.2 %copy-start.2 = (s32[192]{0:T(256)S(1)}, s32[192]{0:T(256)}, u32[]{:S(2)}) copy-start(s32[192]{0:T(256)} %param.12) | copy-start | bytes 2308
  238.3 4.2 %copy-start.3 = (s32[192]{0:T(256)S(1)}, s32[192]{0:T(256)}, u32[]{:S(2)}) copy-start(s32[192]{0:T(256)} %param.11) | copy-start | bytes 2308
  340.2 47.0 %copy-start.1 = (bf16[4,256,256]{2,1,0:T(8,128)(2,1)S(1)}, bf16[4,256,256]{2,1,0:T(8,128)(2,1)}, u32[]{:S(2)}) copy-start(bf16[4,256,256]{2,1,0:T(8,128)(2,1)} %param.9) | copy-start | bytes 1572868
Sparse Core Ops, SparseCore 0:
  346.4 38.7 reduce-scatter.1
